TPU v7x, 32 devices: a whole 2x2x4 slice. The times are simulated.
32 devices in a mesh: dp: 8 (over z, y), expert: 4 (over x, core).
Axes of the slice: x: 2, y: 2, z: 4, core: 2. Of those that a mesh axis runs over, the one named last changes fastest.
Arguments:
- gradients: bfloat16 [8, 128, 128, 128], P('dp', 'expert'), may hold values from -600 to 600
- owner_table: int32 [4, 32], P('expert'), may hold values from 0 to 31, as said below
- step_count: int32 [1], replicated, may hold values from 1 to 8
- master: float32 [128, 128, 128], P(('dp', 'expert')), may hold values from -0.078125 to 0.078125
- first_code: bfloat16 [128, 128, 128], P(('dp', 'expert')), may hold values from -1 to 1
- first_scale: float32 [128], P(('dp', 'expert')), may hold values from 0.1 to 1
- first_power: float32 [128], P(('dp', 'expert')), may hold values from 1 to 3
- second_code: bfloat16 [128, 128, 128], P(('dp', 'expert')), may hold values from 0.0099487305 to 1
- second_scale: float32 [128], P(('dp', 'expert')), may hold values from 0.1 to 2
- second_power: float32 [128], P(('dp', 'expert')), may hold values from 1 to 3
Outputs:
- new_master: float32 [128, 128, 128], P(('dp', 'expert'))
- new_first_code: bfloat16 [128, 128, 128], P(('dp', 'expert'))
- new_first_scale: float32 [128], P(('dp', 'expert'))
- new_first_power: float32 [128], P(('dp', 'expert'))
- new_second_code: bfloat16 [128, 128, 128], P(('dp', 'expert'))
- new_second_scale: float32 [128], P(('dp', 'expert'))
- new_second_power: float32 [128], P(('dp', 'expert'))
- weight_code: bfloat16 [128, 128, 128], P('dp')
- weight_scale: bfloat16 [128], P('dp')
Inputs may be any that keep to these rules, and one draw needn't show every extreme that they name: `owner_table`: each row is a permutation of 0 to 31.
All inputs are finite; a program needn't handle non-finite values. Where the computation divides by a largest or mean magnitude, that divisor is 1e-20 or more.
Results may differ from a plain program's by a relative error of at most 0.009.
Values may be sent and summed in bfloat16 or wider, within the bound.
A program may use at most 128 MiB of HBM per device.

v0:
```python
import jax
import jax.numpy as jnp
from jax import lax
from jax.sharding import PartitionSpec as P

BETA_ONE = 0.9
BETA_TWO = 0.95
LEARN_RATE = 0.01
WEIGHT_DECAY = 0.1
CLIP_RMS = 0.5
LOG_SPAN = 4.0
EPSILON = 1e-06
ADAM_EPS = 1e-08


def decode_moment(code, scale, power):
    values = code.astype(jnp.float32)
    magnitude = jnp.power(jnp.abs(values), 1.0 / power[:, None, None])
    return scale[:, None, None] * jnp.sign(values) * magnitude


def encode_moment(values):
    absval = jnp.abs(values)
    largest = jnp.max(absval, axis=(1, 2))
    average = jnp.mean(absval, axis=(1, 2))
    power = jnp.clip(LOG_SPAN / jnp.log(1.0 + largest / (average + EPSILON)), 1.0, 3.0)
    scale = largest + EPSILON
    scaled = absval / scale[:, None, None]
    coded = (jnp.sign(values) * jnp.power(scaled, power[:, None, None])).astype(jnp.bfloat16)
    return (coded, scale, power)


def finish(
    owned_grad,
    total_sq,
    numel,
    step_count,
    master,
    first_code,
    first_scale,
    first_power,
    second_code,
    second_scale,
    second_power,
):
    clip_factor = jnp.minimum(1.0, CLIP_RMS / jnp.sqrt(total_sq / numel + EPSILON))
    grad = owned_grad * clip_factor
    first_old = decode_moment(first_code, first_scale, first_power)
    second_old = decode_moment(second_code, second_scale, second_power)
    first = BETA_ONE * first_old + (1.0 - BETA_ONE) * grad
    second = BETA_TWO * second_old + (1.0 - BETA_TWO) * grad * grad
    tcount = step_count[0].astype(jnp.float32)
    bias_one = 1.0 - jnp.power(BETA_ONE, tcount)
    bias_two = 1.0 - jnp.power(BETA_TWO, tcount)
    update = first / bias_one / (jnp.sqrt(second / bias_two) + ADAM_EPS)
    new_master = master - LEARN_RATE * (update + WEIGHT_DECAY * master)
    first_out = encode_moment(first)
    second_out = encode_moment(second)
    weight_scale = (jnp.max(jnp.abs(new_master), axis=(1, 2)) + EPSILON).astype(jnp.bfloat16)
    weight_code = (new_master / weight_scale.astype(jnp.float32)[:, None, None]).astype(
        jnp.bfloat16
    )
    return (new_master, first_out, second_out, weight_code, weight_scale)


def replica_total(received):
    return jnp.sum(received, axis=0, dtype=jnp.float32)


def on_device(
    gradients,
    owner_table,
    step_count,
    master,
    first_code,
    first_scale,
    first_power,
    second_code,
    second_scale,
    second_power,
):
    owned_count = master.shape[0]
    tile_side = master.shape[1]
    table_row = owner_table[0]
    numel = float(
        owned_count * lax.axis_size("dp") * lax.axis_size("expert") * tile_side * tile_side
    )
    permuted = jnp.take(gradients[0], table_row, axis=0)
    by_owner = permuted.reshape((lax.axis_size("dp"), owned_count, tile_side, tile_side))
    owned_grad = replica_total(
        lax.all_to_all(by_owner, "dp", split_axis=0, concat_axis=0, tiled=True)
    )
    total_sq = lax.psum(jnp.sum(owned_grad * owned_grad), ("dp", "expert"))
    new_master, first_out, second_out, weight_code, weight_scale = finish(
        owned_grad,
        total_sq,
        numel,
        step_count,
        master,
        first_code,
        first_scale,
        first_power,
        second_code,
        second_scale,
        second_power,
    )
    gathered_code, gathered_scale = (
        lax.all_gather(weight_code, "expert", axis=0, tiled=True),
        lax.all_gather(weight_scale, "expert", axis=0, tiled=True),
    )
    return (
        new_master,
        first_out[0],
        first_out[1],
        first_out[2],
        second_out[0],
        second_out[1],
        second_out[2],
        gathered_code,
        gathered_scale,
    )


def solution(mesh):
    in_specs = (
        P("dp", "expert", None, None),
        P("expert", None),
        P(),
        P(("dp", "expert"), None, None),
        P(("dp", "expert"), None, None),
        P(("dp", "expert")),
        P(("dp", "expert")),
        P(("dp", "expert"), None, None),
        P(("dp", "expert")),
        P(("dp", "expert")),
    )
    out_specs = (
        P(("dp", "expert"), None, None),
        P(("dp", "expert"), None, None),
        P(("dp", "expert")),
        P(("dp", "expert")),
        P(("dp", "expert"), None, None),
        P(("dp", "expert")),
        P(("dp", "expert")),
        P("dp", None, None),
        P("dp"),
    )
    return jax.shard_map(
        on_device, mesh=mesh, in_specs=in_specs, out_specs=out_specs, check_vma=False
    )
```

profile of v0, /device:TPU:0, one launch (start us, length us, event | category | flops | bytes accessed | tf_op | source)
XLA Modules:
  0.0 97.7 jit_solution(17288434971370272178)
XLA Ops:
  0.6 0.0 copy-start
  0.7 0.7 fusion.10
  1.4 0.5 broadcast.144
  1.9 1.3 %reduce.3 = s32[32]{0:T(128)S(1)} reduce(s32[1,32]{1,0:T(1,128)} %param.11, s32[]{:T(128)} %broadcast.144), dimensions={0}, to_apply=%param.11.reduce_sub_computation.3 | reduce | bytes 260 | tf_op args[1]
  3.2 0.1 squeeze.9
  3.3 0.0 copy-done
  3.3 0.7 gather_fusion
  4.1 1.2 %broadcast_select_fusion = bf16[8,4,128,128]{3,2,1,0:T(8,128)(2,1)} fusion(bf16[8,4,128,128]{3,2,1,0:T(8,128)(2,1)S(1)} %bitcast.10, pred[8,4]{1,0:T(8,128)(4,1)S(1)} %compare_and_fusion), kind=kLoop, calls=%fused_computation.2 | loop fusion | flops 524288 | bytes 2097184 | tf_op jit(solution)/shard_map/jit(_take)/select_n | solution.py:88
  5.3 0.0 copy-start.13
  5.3 0.0 copy-start.11
  5.3 0.0 copy-start.12
  5.3 7.4 %all-to-all-start = ((bf16[8,4,128,128]{3,2,1,0:T(8,128)(2,1)}), bf16[8,4,128,128]{3,2,1,0:T(8,128)(2,1)S(1)}, u32[]{:S(2)}, u32[]{:S(2)}) async-start(bf16[8,4,128,128]{3,2,1,0:T(8,128)(2,1)} %broadcast_select_fusion), calls=%async_computation | async-start | bytes 2097152 | tf_op jit(solution)/shard_map/all_to_all | solution.py:91
  12.7 0.0 copy-start.2
  12.7 0.0 copy-start.3
  12.7 0.0 copy-start.4
  12.7 0.0 copy-start.9
  12.7 0.0 copy-start.10
  13.5 0.0 copy-done.13
  13.5 0.6 dynamic-slice
  14.1 0.0 copy-done.11
  14.1 0.0 copy-done.12
  14.2 24.3 %all-to-all-done = bf16[8,4,128,128]{3,2,1,0:T(8,128)(2,1)S(1)} async-done(((bf16[8,4,128,128]{3,2,1,0:T(8,128)(2,1)}), bf16[8,4,128,128]{3,2,1,0:T(8,128)(2,1)S(1)}, u32[]{:S(2)}, u32[]{:S(2)}) %all-to-all-start) | async-done | bytes 1048608 | tf_op jit(solution)/shard_map/all_to_all | solution.py:91
  38.5 0.1 convert_reduce_fusion
  38.6 0.7 multiply_reduce_fusion
  39.9 38.0 %psum.7 = f32[]{:T(128)} all-reduce(f32[]{:T(128)} %multiply_reduce_fusion), channel_id=1, replica_groups=mesh['dp'=8,'expert'=4] {'dp','expert'}, use_global_device_ids=true, to_apply=%region_2.3 | all-reduce | flops 1 | bytes 8 | tf_op jit(solution)/shard_map/psum | solution.py:93
  78.6 0.0 copy-done.2
  78.6 0.0 copy-done.3
  78.6 0.0 copy-done.4
  78.6 0.0 copy-done.9
  78.6 0.0 copy-done.10
  78.6 1.1 %abs_reduce_fusion = (f32[4]{0:T(128)S(1)}, f32[4,128,128]{2,1,0:T(8,128)S(1)}, f32[4,128,128]{2,1,0:T(8,128)S(1)}, f32[4,128,128]{2,1,0:T(8,128)S(1)}) fusion(f32[4,128,128]{2,1,0:T(8,128)S(1)} %copy-done.2, f32[]{:T(128)} %bitcast.5, f32[]{:T(128)} %bitcast.4, f32[4,128,128]{2,1,0:T(8,128)S(1)} %convert_reduce_fusion, f32[]{:T(128)S(6)} %min.15, ...), kind=kLoop, calls=%fused_computation.19 | loop fusion | flops 1835004 | bytes 1572956 | tf_op jit(solution)/shard_map/reduce_max | solution.py:59
  79.7 0.0 copy-start.1
  79.7 0.1 abs_reduce_fusion.3
  79.9 0.1 abs_reduce_fusion.1
  80.0 0.1 divide_convert_fusion
  80.1 8.0 %all_gather.6 = bf16[16,128,128]{2,1,0:T(8,128)(2,1)S(1)} all-gather(bf16[4,128,128]{2,1,0:T(8,128)(2,1)S(1)} %divide_convert_fusion), channel_id=1, replica_groups=mesh['dp'=8,'expert'=4] {'expert'}, dimensions={0}, use_global_device_ids=true | all-gather | bytes 655360 | tf_op jit(solution)/shard_map/all_gather | solution.py:108
  88.1 0.2 dynamic-update-slice
  88.2 6.9 %all-reduce = bf16[16]{0:T(256)(128)(2,1)} all-reduce(bf16[16]{0:T(256)(128)(2,1)S(1)} %dynamic-update-slice), channel_id=1, replica_groups=mesh['dp'=8,'expert'=4] {'expert'}, use_global_device_ids=true, to_apply=%add | all-reduce | flops 16 | bytes 64
  95.2 0.0 copy-start.5
  95.2 0.0 copy-start.6
  95.2 0.0 copy-start.7
  95.2 0.0 copy-start.8
  95.2 1.6 %multiply_convert_fusion = (bf16[4,128,128]{2,1,0:T(8,128)(2,1)}, bf16[4,128,128]{2,1,0:T(8,128)(2,1)}) fusion(f32[4,128,128]{2,1,0:T(8,128)S(1)} %get-tuple-element.15, f32[4]{0:T(128)S(1)} %get-tuple-element.40, f32[4]{0:T(128)S(1)} %get-tuple-element.39, f32[4]{0:T(128)S(1)} %get-tuple-element.37, f32[4]{0:T(128)S(1)} %get-tuple-element.36, ...), kind=kLoop, calls=%fused_computation.20 | loop fusion | flops 655360 | bytes 786496 | tf_op jit(solution)/shard_map/convert_element_type | solution.py:29
  96.9 0.0 copy-done.1
  96.9 0.8 copy.22
  97.7 0.0 copy-done.5
  97.7 0.0 copy-done.6
  97.7 0.0 copy-done.7
  97.7 0.0 copy-done.8
  (8 shorter events, 0.1 us)
Async XLA Ops:
  0.6 2.7 %copy-start = (bf16[1,32,128,128]{3,2,1,0:T(8,128)(2,1)S(1)}, bf16[1,32,128,128]{3,2,1,0:T(8,128)(2,1)}, u32[]{:S(2)}) copy-start(bf16[1,32,128,128]{3,2,1,0:T(8,128)(2,1)} %param.10) | copy-start | bytes 3145732
  5.3 8.3 %copy-start.13 = (u32[32]{0:T(128)S(1)}, u32[32]{0:T(128)}, u32[]{:S(2)}) copy-start(u32[32]{0:T(128)} %constant.72) | copy-start | bytes 388
  5.3 8.9 %copy-start.11 = (f32[4]{0:T(128)S(1)}, f32[4]{0:T(128)}, u32[]{:S(2)}) copy-start(f32[4]{0:T(128)} %param.19) | copy-start | bytes 52
  5.3 8.9 %copy-start.12 = (f32[4]{0:T(128)S(1)}, f32[4]{0:T(128)}, u32[]{:S(2)}) copy-start(f32[4]{0:T(128)} %param.16) | copy-start | bytes 52
  5.3 33.2 %all-to-all-start = ((bf16[8,4,128,128]{3,2,1,0:T(8,128)(2,1)}), bf16[8,4,128,128]{3,2,1,0:T(8,128)(2,1)S(1)}, u32[]{:S(2)}, u32[]{:S(2)}) async-start(bf16[8,4,128,128]{3,2,1,0:T(8,128)(2,1)} %broadcast_select_fusion), calls=%async_computation | async-start | bytes 2097152 | tf_op jit(solution)/shard_map/all_to_all | solution.py:91
  12.7 65.9 %copy-start.2 = (f32[4,128,128]{2,1,0:T(8,128)S(1)}, f32[4,128,128]{2,1,0:T(8,128)}, u32[]{:S(2)}) copy-start(f32[4,128,128]{2,1,0:T(8,128)} %param.13) | copy-start | bytes 786436
  12.7 65.9 %copy-start.3 = (bf16[4,128,128]{2,1,0:T(8,128)(2,1)S(1)}, bf16[4,128,128]{2,1,0:T(8,128)(2,1)}, u32[]{:S(2)}) copy-start(bf16[4,128,128]{2,1,0:T(8,128)(2,1)} %param.17) | copy-start | bytes 393220
  12.7 65.9 %copy-start.4 = (bf16[4,128,128]{2,1,0:T(8,128)(2,1)S(1)}, bf16[4,128,128]{2,1,0:T(8,128)(2,1)}, u32[]{:S(2)}) copy-start(bf16[4,128,128]{2,1,0:T(8,128)(2,1)} %param.14) | copy-start | bytes 393220
  12.7 65.9 %copy-start.9 = (f32[4]{0:T(128)S(1)}, f32[4]{0:T(128)}, u32[]{:S(2)}) copy-start(f32[4]{0:T(128)} %param.18) | copy-start | bytes 52
  12.7 65.9 %copy-start.10 = (f32[4]{0:T(128)S(1)}, f32[4]{0:T(128)}, u32[]{:S(2)}) copy-start(f32[4]{0:T(128)} %param.15) | copy-start | bytes 52
  79.7 17.2 %copy-start.1 = (f32[4,128,128]{2,1,0:T(8,128)}, f32[4,128,128]{2,1,0:T(8,128)S(1)}, u32[]{:S(2)}) copy-start(f32[4,128,128]{2,1,0:T(8,128)S(1)} %get-tuple-element.34) | copy-start | bytes 786436
  95.2 2.5 %copy-start.5 = (f32[4]{0:T(128)}, f32[4]{0:T(128)S(1)}, u32[]{:S(2)}) copy-start(f32[4]{0:T(128)S(1)} %get-tuple-element.36) | copy-start | bytes 52
  95.2 2.5 %copy-start.6 = (f32[4]{0:T(128)}, f32[4]{0:T(128)S(1)}, u32[]{:S(2)}) copy-start(f32[4]{0:T(128)S(1)} %get-tuple-element.37) | copy-start | bytes 52
  95.2 2.5 %copy-start.7 = (f32[4]{0:T(128)}, f32[4]{0:T(128)S(1)}, u32[]{:S(2)}) copy-start(f32[4]{0:T(128)S(1)} %get-tuple-element.39) | copy-start | bytes 52
  95.2 2.5 %copy-start.8 = (f32[4]{0:T(128)}, f32[4]{0:T(128)S(1)}, u32[]{:S(2)}) copy-start(f32[4]{0:T(128)S(1)} %get-tuple-element.40) | copy-start | bytes 52
where the time goes:
time: 98.1 us; the launch traced here: 97.7 us
  blocking collectives  52.8 us (54%)
  waiting for transfers between devices  24.3 us (25%)
  starting transfers between devices  7.44 us (8%)
  other arithmetic  7.16 us (7%)
  local copies, waits for them, and re-layouts  2.99 us (3%)
  between operations  2.95 us (3%)
    psum x1, blocking collectives, on_device(): total_sq = lax.psum(jnp.sum(owned_grad * owned_grad), ('dp', 'expert'))  38 us
    all_to_all x1, waiting for transfers between devices, on_device(): lax.all_to_all(by_owner, 'dp', split_axis=0, concat_axis=0, tiled=True)  24.3 us
    all_gather x1, blocking collectives, on_device(): lax.all_gather(weight_code, 'expert', axis=0, tiled=True)  7.96 us
    all_to_all x1, starting transfers between devices, on_device(): lax.all_to_all(by_owner, 'dp', split_axis=0, concat_axis=0, tiled=True)  7.44 us
    unnamed x1, blocking collectives  6.9 us
    unnamed x33, local copies, waits for them, and re-layouts  2.16 us
  transfers between devices with their start and end apart: 1, of which 1 were waited for; matrix products, arithmetic and copies ran while one was open for 1% of the time, Pallas kernels for 0%

commit v1 on v0

v1 whole, which is shorter than its diff:
```python
import functools
import math

import jax
import jax.numpy as jnp
from jax import lax
from jax.experimental import pallas as pl
from jax.experimental.pallas import tpu as pltpu
from jax.sharding import PartitionSpec as P

BETA_ONE = 0.9
BETA_TWO = 0.95
LEARN_RATE = 0.01
WEIGHT_DECAY = 0.1
CLIP_RMS = 0.5
LOG_SPAN = 4.0
EPSILON = 1e-06
ADAM_EPS = 1e-08

MESH = pl.DeviceIdType.MESH


def flip(index, mask):
    out = index
    bit = 1
    while bit <= mask:
        if mask & bit:
            out = out + bit * (1 - 2 * ((index // bit) % 2))
        bit *= 2
    return out


def bits_of(count):
    bits = []
    bit = 1
    while bit < count:
        bits.append(bit)
        bit *= 2
    return bits


def slots_of(count):
    base, bases = 0, {}
    for bit in bits_of(count):
        bases[bit] = base
        base += count // (2 * bit)
    return bases, base


def low_bit(number):
    return number & -number


def signed_power(values, logs, power):
    magnitude = jnp.where(values == 0.0, 0.0, jnp.exp(logs * power))
    return jnp.where(values < 0.0, -magnitude, magnitude)


def tile_max(values):
    return jnp.max(jnp.max(values, axis=0, keepdims=True), axis=1, keepdims=True)


def tile_sum(values):
    return jnp.sum(jnp.sum(values, axis=0, keepdims=True), axis=1, keepdims=True)


def kernel(
    ranks,
    experts,
    own,
    numel,
    table,
    step_count,
    first_scale,
    first_power,
    second_scale,
    second_power,
    grad_hbm,
    master_hbm,
    first_hbm,
    second_hbm,
    new_master_out,
    first_out,
    second_out,
    weight_out,
    first_scale_out,
    first_power_out,
    second_scale_out,
    second_power_out,
    weight_scale_out,
    gbuf,
    sendbuf,
    recvbuf,
    acc,
    master,
    first_in,
    second_in,
    first,
    second,
    first_code,
    second_code,
    weights,
    sums_expert,
    sums_rank,
    load_sem,
    store_sem,
    send_sem,
    recv_sem,
    sum_send,
    sum_recv,
    gather_send,
    gather_recv,
    scale_send,
    scale_recv,
):
    me = lax.axis_index("dp")
    expert = lax.axis_index("expert")
    side = acc.shape[1]
    bases, _ = slots_of(ranks)

    loads = [
        pltpu.make_async_copy(grad_hbm.at[0], gbuf, load_sem.at[0]),
        pltpu.make_async_copy(first_hbm, first_in, load_sem.at[1]),
        pltpu.make_async_copy(second_hbm, second_in, load_sem.at[2]),
        pltpu.make_async_copy(master_hbm, master, load_sem.at[3]),
    ]
    loads[0].start()

    barrier = pltpu.get_barrier_semaphore()
    for r in range(1, ranks):
        pl.semaphore_signal(
            barrier, inc=1, device_id=(flip(me, r), expert), device_id_type=MESH
        )
    for r in range(1, experts):
        pl.semaphore_signal(
            barrier, inc=1, device_id=(me, flip(expert, r)), device_id_type=MESH
        )
    for load in loads[1:]:
        load.start()

    def mine(r, k):
        return gbuf[table[0, flip(me, r) * own + k]]

    def rank_copy(bit, slot, k):
        at = slot * own + k
        return pltpu.make_async_remote_copy(
            src_ref=sendbuf.at[at],
            dst_ref=recvbuf.at[at],
            send_sem=send_sem.at[slot],
            recv_sem=recv_sem.at[at],
            device_id=(flip(me, bit), expert),
            device_id_type=MESH,
        )

    loads[0].wait()
    groups = list(range(ranks // 2 - 1, -1, -1))
    for j in groups:

        def place(k, carry, j=j):
            sendbuf[(bases[1] + j) * own + k] = mine(2 * j + 1, k)
            return carry

        lax.fori_loop(0, own, place, 0)
    pl.semaphore_wait(barrier, ranks + experts - 2)
    for j in groups:
        for k in range(own):
            rank_copy(1, bases[1] + j, k).start()

    loads[1].wait()
    loads[2].wait()

    def decode(k, carry):
        one = first_in[k].astype(jnp.float32)
        one_power = 1.0 / jnp.full((1, 1), first_power[k], jnp.float32)
        first[k] = (BETA_ONE * first_scale[k]) * signed_power(
            one, jnp.log(jnp.abs(one)), one_power
        )
        two = second_in[k].astype(jnp.float32)
        two_power = 1.0 / jnp.full((1, 1), second_power[k], jnp.float32)
        second[k] = (BETA_TWO * second_scale[k]) * signed_power(
            two, jnp.log(jnp.abs(two)), two_power
        )
        return carry

    lax.fori_loop(0, own, decode, 0)

    square = jnp.zeros((8, side), jnp.float32)
    for j in groups:
        r = 2 * j

        def add(k, carry, r=r):
            total = mine(r, k).astype(jnp.float32)
            for bit in bits_of(ranks):
                if r & bit:
                    slot = bases[bit] + r // (2 * bit)
                    sendbuf[slot * own + k] = total.astype(jnp.bfloat16)
                    rank_copy(bit, slot, k).start()
                    return carry
                slot = bases[bit] + r // (2 * bit)
                rank_copy(bit, slot, k).wait_recv()
                total = total + recvbuf[slot * own + k].astype(jnp.float32)
            acc[k] = total
            return carry + jnp.sum((total * total).reshape(side // 8, 8, side), axis=0)

        square = lax.fori_loop(0, own, add, square)

    def sum_copy(buffer, at, slot, target):
        return pltpu.make_async_remote_copy(
            src_ref=buffer.at[0],
            dst_ref=buffer.at[at],
            send_sem=sum_send.at[slot],
            recv_sem=sum_recv.at[slot],
            device_id=target,
            device_id_type=MESH,
        )

    expert_sums = [
        sum_copy(sums_expert, r, r - 1, (me, flip(expert, r))) for r in range(1, experts)
    ]
    rank_sums = [
        sum_copy(sums_rank, r, experts - 2 + r, (flip(me, r), expert))
        for r in range(1, ranks)
    ]
    sums_expert[0] = jnp.sum(square, axis=0, keepdims=True)
    for copy in expert_sums:
        copy.start()
    for copy in expert_sums:
        copy.wait_recv()
    sums_rank[0] = jnp.sum(sums_expert[...], axis=0)
    for copy in rank_sums:
        copy.start()

    loads[3].wait()
    steps = jnp.full((1, side), step_count[0].astype(jnp.float32), jnp.float32)
    bias_one = (1.0 - jnp.exp(steps * math.log(BETA_ONE)))[:, :1]
    bias_two = (1.0 - jnp.exp(steps * math.log(BETA_TWO)))[:, :1]
    for copy in rank_sums:
        copy.wait_recv()
    total_sq = jnp.sum(jnp.sum(sums_rank[...], axis=0), axis=1, keepdims=True)
    clip_factor = jnp.minimum(1.0, CLIP_RMS / jnp.sqrt(total_sq / numel + EPSILON))

    def gather_copy(r, bit, k):
        at = flip(expert, r) * own + k
        slot = ((r | bit) - 1) * own + k
        return pltpu.make_async_remote_copy(
            src_ref=weights.at[at],
            dst_ref=weights.at[at],
            send_sem=gather_send.at[slot],
            recv_sem=gather_recv.at[slot],
            device_id=(me, flip(expert, bit)),
            device_id_type=MESH,
        )

    def scale_copy(r):
        at = pl.ds(expert * own, own)
        return pltpu.make_async_remote_copy(
            src_ref=weight_scale_out.at[at],
            dst_ref=weight_scale_out.at[at],
            send_sem=scale_send.at[r - 1],
            recv_sem=scale_recv.at[r - 1],
            device_id=(me, flip(expert, r)),
            device_id_type=MESH,
        )

    expert_bits = bits_of(experts)[::-1]

    def finish(k, carry):
        grad = acc[k] * clip_factor
        one = first[k] + (1.0 - BETA_ONE) * grad
        two = second[k] + (1.0 - BETA_TWO) * grad * grad
        first[k] = one
        second[k] = two
        update = one / bias_one / (jnp.sqrt(two / bias_two) + ADAM_EPS)
        old = master[k]
        new = old - LEARN_RATE * (update + WEIGHT_DECAY * old)
        master[k] = new
        scale = (tile_max(jnp.abs(new)) + EPSILON).astype(jnp.bfloat16).astype(jnp.float32)
        weights[expert * own + k] = (new / scale).astype(jnp.bfloat16)
        weight_scale_out[expert * own + k] = jnp.broadcast_to(scale, (1, side))
        for bit in expert_bits:
            gather_copy(0, bit, k).start()
        return carry

    lax.fori_loop(0, own, finish, 0)
    for r in range(1, experts):
        scale_copy(r).start()
    stores = [pltpu.make_async_copy(master, new_master_out, store_sem.at[0])]
    stores[0].start()

    def encode(values, code, scale_out, power_out, k):
        size = jnp.abs(values)
        largest = tile_max(size)
        average = tile_sum(size) * (1.0 / (side * side))
        power = jnp.clip(
            LOG_SPAN / jnp.log(1.0 + largest / (average + EPSILON)), 1.0, 3.0
        )
        scale = largest + EPSILON
        code[k] = signed_power(values, jnp.log(size / scale), power).astype(jnp.bfloat16)
        scale_out[k] = scale[0, 0]
        power_out[k] = power[0, 0]

    def encode_both(k, carry):
        encode(first[k], first_code, first_scale_out, first_power_out, k)
        encode(second[k], second_code, second_scale_out, second_power_out, k)
        return carry

    lax.fori_loop(0, own, encode_both, 0)
    stores.append(pltpu.make_async_copy(first_code, first_out, store_sem.at[1]))
    stores.append(pltpu.make_async_copy(second_code, second_out, store_sem.at[2]))
    stores[1].start()
    stores[2].start()

    order = [0]
    for bit in expert_bits:
        order = order + [r | bit for r in order]
    for r in order[1:]:
        last = low_bit(r)
        for k in range(own):
            gather_copy(r - last, last, k).wait_recv()
            for bit in expert_bits:
                if bit < last:
                    gather_copy(r, bit, k).start()
    for r in range(1, experts):
        scale_copy(r).wait_recv()
    stores.append(pltpu.make_async_copy(weights, weight_out, store_sem.at[3]))
    stores[3].start()

    for bit in bits_of(ranks):
        for j in range(ranks // (2 * bit)):
            slot = bases[bit] + j
            tiles = pl.ds(slot * own, own)
            pltpu.make_async_remote_copy(
                src_ref=sendbuf.at[tiles],
                dst_ref=recvbuf.at[tiles],
                send_sem=send_sem.at[slot],
                recv_sem=recv_sem.at[slot * own],
                device_id=(flip(me, bit), expert),
                device_id_type=MESH,
            ).wait_send()
    for copy in expert_sums + rank_sums:
        copy.wait_send()
    for r in order[1:]:
        for k in range(own):
            gather_copy(r - low_bit(r), low_bit(r), k).wait_send()
    for r in range(1, experts):
        scale_copy(r).wait_send()
    for store in stores:
        store.wait()


def on_device(
    gradients,
    owner_table,
    step_count,
    master,
    first_code,
    first_scale,
    first_power,
    second_code,
    second_scale,
    second_power,
):
    ranks, experts = lax.axis_size("dp"), lax.axis_size("expert")
    own, side = master.shape[0], master.shape[1]
    block = gradients.shape[1]
    numel = float(own * ranks * experts * side * side)
    _, slots = slots_of(ranks)
    tiles = (own, side, side)
    smem = pl.BlockSpec(memory_space=pltpu.SMEM)
    vmem = pl.BlockSpec(memory_space=pltpu.VMEM)
    hbm = pl.BlockSpec(memory_space=pl.ANY)
    small = jax.ShapeDtypeStruct((own,), jnp.float32)
    dma = pltpu.SemaphoreType.DMA
    out = pl.pallas_call(
        functools.partial(kernel, ranks, experts, own, numel),
        out_shape=(
            jax.ShapeDtypeStruct(tiles, jnp.float32),
            jax.ShapeDtypeStruct(tiles, jnp.bfloat16),
            jax.ShapeDtypeStruct(tiles, jnp.bfloat16),
            jax.ShapeDtypeStruct((experts * own, side, side), jnp.bfloat16),
            small,
            small,
            small,
            small,
            jax.ShapeDtypeStruct((experts * own, 1, side), jnp.float32),
        ),
        in_specs=[smem] * 6 + [hbm] * 4,
        out_specs=(hbm,) * 4 + (smem,) * 4 + (vmem,),
        scratch_shapes=[
            pltpu.VMEM((block, side, side), jnp.bfloat16),
            pltpu.VMEM((slots * own, side, side), jnp.bfloat16),
            pltpu.VMEM((slots * own, side, side), jnp.bfloat16),
            pltpu.VMEM(tiles, jnp.float32),
            pltpu.VMEM(tiles, jnp.float32),
            pltpu.VMEM(tiles, jnp.bfloat16),
            pltpu.VMEM(tiles, jnp.bfloat16),
            pltpu.VMEM(tiles, jnp.float32),
            pltpu.VMEM(tiles, jnp.float32),
            pltpu.VMEM(tiles, jnp.bfloat16),
            pltpu.VMEM(tiles, jnp.bfloat16),
            pltpu.VMEM((experts * own, side, side), jnp.bfloat16),
            pltpu.VMEM((experts, 1, side), jnp.float32),
            pltpu.VMEM((ranks, 1, side), jnp.float32),
            dma((4,)),
            dma((4,)),
            dma((slots,)),
            dma((slots * own,)),
            dma((experts + ranks - 2,)),
            dma((experts + ranks - 2,)),
            dma(((experts - 1) * own,)),
            dma(((experts - 1) * own,)),
            dma((experts - 1,)),
            dma((experts - 1,)),
        ],
        compiler_params=pltpu.CompilerParams(
            collective_id=0, has_side_effects=True, vmem_limit_bytes=48 << 20
        ),
    )(
        owner_table,
        step_count,
        first_scale,
        first_power,
        second_scale,
        second_power,
        gradients,
        master,
        first_code,
        second_code,
    )
    new_master, first_new, second_new, weights = out[:4]
    scales = out[8][:, 0, 0].astype(jnp.bfloat16)
    return (
        new_master,
        first_new,
        out[4],
        out[5],
        second_new,
        out[6],
        out[7],
        weights,
        scales,
    )


def solution(mesh):
    in_specs = (
        P("dp", "expert", None, None),
        P("expert", None),
        P(),
        P(("dp", "expert"), None, None),
        P(("dp", "expert"), None, None),
        P(("dp", "expert")),
        P(("dp", "expert")),
        P(("dp", "expert"), None, None),
        P(("dp", "expert")),
        P(("dp", "expert")),
    )
    out_specs = (
        P(("dp", "expert"), None, None),
        P(("dp", "expert"), None, None),
        P(("dp", "expert")),
        P(("dp", "expert")),
        P(("dp", "expert"), None, None),
        P(("dp", "expert")),
        P(("dp", "expert")),
        P("dp", None, None),
        P("dp"),
    )
    return jax.shard_map(
        on_device, mesh=mesh, in_specs=in_specs, out_specs=out_specs, check_vma=False
    )
```

time: 98.1 us -> 45.3 us (0.46)
  blocking collectives: 52.8 us -> 0 us
  Pallas kernels: 0 us -> 32.8 us
  waiting for transfers between devices: 24.3 us -> 0 us
  local copies, waits for them, and re-layouts: 2.99 us -> 10.9 us
  starting transfers between devices: 7.44 us -> 0 us
  other arithmetic: 7.16 us -> 0 us
  between operations: 2.95 us -> 1.39 us
    psum x1 -> x0, blocking collectives: 38 us -> none  [on_device(): total_sq = lax.psum(jnp.sum(owned_grad * owned_grad), ('dp', 'expert'))]
    pallas_call x0 -> x1, Pallas kernels: none -> 32.8 us  [on_device(): pl.pallas_call(functools.partial(kernel, ranks, experts, own, numel), out...]
    all_to_all x1 -> x0, waiting for transfers between devices: 24.3 us -> none  [on_device(): lax.all_to_all(by_owner, 'dp', split_axis=0, concat_axis=0, tiled=True)]
    unnamed x33 -> x26, local copies, waits for them, and re-layouts: 2.16 us -> 10.1 us
    all_gather x1 -> x0, blocking collectives: 7.96 us -> none  [on_device(): lax.all_gather(weight_code, 'expert', axis=0, tiled=True)]
    all_to_all x1 -> x0, starting transfers between devices: 7.44 us -> none  [on_device(): lax.all_to_all(by_owner, 'dp', split_axis=0, concat_axis=0, tiled=True)]
    unnamed x1 -> x0, blocking collectives: 6.9 us -> none
    select_n x2 -> x0, other arithmetic: 1.9 us -> none  [on_device(): permuted = jnp.take(gradients[0], table_row, axis=0)]
  transfers between devices with their start and end apart: 1 -> 0, of which waited for: 1 -> 0; matrix products, arithmetic and copies ran while one was open for 1% -> 0% of each run, Pallas kernels for 0% -> 0%
where the time goes in v1:
time: 45.3 us; the launch traced here: 45 us
  Pallas kernels  32.8 us (72%)
  local copies, waits for them, and re-layouts  10.9 us (24%)
  between operations  1.39 us (3%)
    pallas_call x1, Pallas kernels, on_device(): pl.pallas_call(functools.partial(kernel, ranks, experts, own, numel), out...  32.8 us
    unnamed x26, local copies, waits for them, and re-layouts  10.1 us

profile of v1, /device:TPU:0, one launch (start us, length us, event | category | flops | bytes accessed | tf_op | source)
XLA Modules:
  0.0 45.0 jit_solution(8749147150814324267)
XLA Ops:
  0.6 0.0 copy-start.6
  0.7 0.0 copy-start.5
  0.7 0.0 copy-start.4
  1.3 0.0 copy-done.6
  1.4 0.0 copy-done.5
  1.4 0.0 copy-done.4
  1.4 0.0 copy-start
  1.4 1.2 %copy-done = bf16[1,32,128,128]{3,2,1,0:T(8,128)(2,1)S(1)} copy-done((bf16[1,32,128,128]{3,2,1,0:T(8,128)(2,1)S(1)}, bf16[1,32,128,128]{3,2,1,0:T(8,128)(2,1)}, u32[]{:S(2)}) %copy-start) | copy-done | bytes 1048600
  2.6 0.0 copy-start.1
  2.6 0.9 %copy-done.1 = f32[4,128,128]{2,1,0:T(8,128)S(1)} copy-done((f32[4,128,128]{2,1,0:T(8,128)S(1)}, f32[4,128,128]{2,1,0:T(8,128)}, u32[]{:S(2)}) %copy-start.1) | copy-done | bytes 262168
  3.6 0.0 copy-start.2
  3.6 0.9 %copy-done.2 = bf16[4,128,128]{2,1,0:T(8,128)(2,1)S(1)} copy-done((bf16[4,128,128]{2,1,0:T(8,128)(2,1)S(1)}, bf16[4,128,128]{2,1,0:T(8,128)(2,1)}, u32[]{:S(2)}) %copy-start.2) | copy-done | bytes 131096
  4.5 0.0 copy-start.3
  4.5 0.9 %copy-done.3 = bf16[4,128,128]{2,1,0:T(8,128)(2,1)S(1)} copy-done((bf16[4,128,128]{2,1,0:T(8,128)(2,1)S(1)}, bf16[4,128,128]{2,1,0:T(8,128)(2,1)}, u32[]{:S(2)}) %copy-start.3) | copy-done | bytes 131096
  5.4 0.0 copy-start.7
  5.4 0.7 %copy-done.7 = f32[4]{0:T(128)S(1)} copy-done((f32[4]{0:T(128)S(1)}, f32[4]{0:T(128)}, u32[]{:S(2)}) %copy-start.7) | copy-done | bytes 40
  6.0 0.0 copy-start.8
  6.0 0.7 %copy-done.8 = f32[4]{0:T(128)S(1)} copy-done((f32[4]{0:T(128)S(1)}, f32[4]{0:T(128)}, u32[]{:S(2)}) %copy-start.8) | copy-done | bytes 40
  6.7 32.8 %shard_map.169 = (f32[4,128,128]{2,1,0:T(8,128)S(1)}, bf16[4,128,128]{2,1,0:T(8,128)(2,1)S(1)}, bf16[4,128,128]{2,1,0:T(8,128)(2,1)S(1)}, bf16[16,128,128]{2,1,0...) custom-call(s32[1,32]{1,0:T(1,128)S(1)} %copy-done.4, ...), custom_call_target="tpu_custom_call" | custom-call | tf_op jit(solution)/shard_map/pallas_call | solution.py:374
  39.4 0.7 %fusion = bf16[16]{0:T(256)(128)(2,1)} fusion(f32[16,1,128]{2,1,0:T(1,128)S(1)} %get-tuple-element.26), kind=kLoop, calls=%fused_computation.1 | loop fusion | bytes 64 | tf_op jit(solution)/shard_map/slice | solution.py:431
  40.2 0.7 %copy.28 = f32[4,128,128]{2,1,0:T(8,128)} copy(f32[4,128,128]{2,1,0:T(8,128)S(1)} %get-tuple-element.36) | data formatting | bytes 524288
  40.9 0.7 %copy.29 = bf16[4,128,128]{2,1,0:T(8,128)(2,1)} copy(bf16[4,128,128]{2,1,0:T(8,128)(2,1)S(1)} %get-tuple-element.37) | data formatting | bytes 262144
  41.5 0.5 %copy.30 = f32[4]{0:T(128)} copy(f32[4]{0:T(128)S(1)} %get-tuple-element.38) | data formatting | bytes 32
  42.0 0.5 %copy.31 = f32[4]{0:T(128)} copy(f32[4]{0:T(128)S(1)} %get-tuple-element.39) | data formatting | bytes 32
  42.5 0.7 %copy.32 = bf16[4,128,128]{2,1,0:T(8,128)(2,1)} copy(bf16[4,128,128]{2,1,0:T(8,128)(2,1)S(1)} %get-tuple-element.40) | data formatting | bytes 262144
  43.2 0.5 %copy.33 = f32[4]{0:T(128)} copy(f32[4]{0:T(128)S(1)} %get-tuple-element.41) | data formatting | bytes 32
  43.7 0.5 %copy.34 = f32[4]{0:T(128)} copy(f32[4]{0:T(128)S(1)} %get-tuple-element.42) | data formatting | bytes 32
  44.2 0.8 %copy.35 = bf16[16,128,128]{2,1,0:T(8,128)(2,1)} copy(bf16[16,128,128]{2,1,0:T(8,128)(2,1)S(1)} %get-tuple-element.43) | data formatting | bytes 1048576
Async XLA Ops:
  0.6 0.7 %copy-start.6 = (f32[4]{0:T(128)S(1)}, f32[4]{0:T(128)}, u32[]{:S(2)}) copy-start(f32[4]{0:T(128)} %first_power.1) | copy-start | bytes 52
  0.7 0.7 %copy-start.5 = (f32[4]{0:T(128)S(1)}, f32[4]{0:T(128)}, u32[]{:S(2)}) copy-start(f32[4]{0:T(128)} %first_scale.1) | copy-start | bytes 52
  0.7 0.7 %copy-start.4 = (s32[1,32]{1,0:T(1,128)S(1)}, s32[1,32]{1,0:T(1,128)}, u32[]{:S(2)}) copy-start(s32[1,32]{1,0:T(1,128)} %table.1) | copy-start | bytes 388
  1.4 1.2 %copy-start = (bf16[1,32,128,128]{3,2,1,0:T(8,128)(2,1)S(1)}, bf16[1,32,128,128]{3,2,1,0:T(8,128)(2,1)}, u32[]{:S(2)}) copy-start(bf16[1,32,128,128]{3,2,1,0:T(8,128)(2,1)} %grad_hbm.1) | copy-start | bytes 3145732
  2.6 0.9 %copy-start.1 = (f32[4,128,128]{2,1,0:T(8,128)S(1)}, f32[4,128,128]{2,1,0:T(8,128)}, u32[]{:S(2)}) copy-start(f32[4,128,128]{2,1,0:T(8,128)} %master_hbm.1) | copy-start | bytes 786436
  3.6 0.9 %copy-start.2 = (bf16[4,128,128]{2,1,0:T(8,128)(2,1)S(1)}, bf16[4,128,128]{2,1,0:T(8,128)(2,1)}, u32[]{:S(2)}) copy-start(bf16[4,128,128]{2,1,0:T(8,128)(2,1)} %first_hbm.1) | copy-start | bytes 393220
  4.5 0.9 %copy-start.3 = (bf16[4,128,128]{2,1,0:T(8,128)(2,1)S(1)}, bf16[4,128,128]{2,1,0:T(8,128)(2,1)}, u32[]{:S(2)}) copy-start(bf16[4,128,128]{2,1,0:T(8,128)(2,1)} %second_hbm.1) | copy-start | bytes 393220
  5.4 0.7 %copy-start.7 = (f32[4]{0:T(128)S(1)}, f32[4]{0:T(128)}, u32[]{:S(2)}) copy-start(f32[4]{0:T(128)} %second_scale.1) | copy-start | bytes 52
  6.0 0.7 %copy-start.8 = (f32[4]{0:T(128)S(1)}, f32[4]{0:T(128)}, u32[]{:S(2)}) copy-start(f32[4]{0:T(128)} %second_power.1) | copy-start | bytes 52

commit v2 on v1

--- a/solution.py
+++ b/solution.py
@@ -69,41 +69,38 @@
     experts,
     own,
     numel,
+    table_hbm,
+    step_count,
+    first_scale_hbm,
+    first_power_hbm,
+    second_scale_hbm,
+    second_power_hbm,
+    grad_hbm,
+    master_hbm,
+    first_hbm,
+    second_hbm,
+    master,
+    first_code,
+    second_code,
+    weights,
+    stats_out,
+    weight_scale_out,
     table,
-    step_count,
     first_scale,
     first_power,
     second_scale,
     second_power,
-    grad_hbm,
-    master_hbm,
-    first_hbm,
-    second_hbm,
-    new_master_out,
-    first_out,
-    second_out,
-    weight_out,
-    first_scale_out,
-    first_power_out,
-    second_scale_out,
-    second_power_out,
-    weight_scale_out,
     gbuf,
     sendbuf,
     recvbuf,
     acc,
-    master,
     first_in,
     second_in,
     first,
     second,
-    first_code,
-    second_code,
-    weights,
     sums_expert,
     sums_rank,
     load_sem,
-    store_sem,
     send_sem,
     recv_sem,
     sum_send,
@@ -124,6 +121,19 @@
         pltpu.make_async_copy(second_hbm, second_in, load_sem.at[2]),
         pltpu.make_async_copy(master_hbm, master, load_sem.at[3]),
     ]
+    scalars = [
+        pltpu.make_async_copy(src, dst, load_sem.at[4 + i])
+        for i, (src, dst) in enumerate(
+            (
+                (table_hbm, table),
+                (first_scale_hbm, first_scale),
+                (first_power_hbm, first_power),
+                (second_scale_hbm, second_scale),
+                (second_power_hbm, second_power),
+            )
+        )
+    ]
+    scalars[0].start()
     loads[0].start()
 
     barrier = pltpu.get_barrier_semaphore()
@@ -135,7 +145,7 @@
         pl.semaphore_signal(
             barrier, inc=1, device_id=(me, flip(expert, r)), device_id_type=MESH
         )
-    for load in loads[1:]:
+    for load in scalars[1:] + loads[1:]:
         load.start()
 
     def mine(r, k):
@@ -152,6 +162,7 @@
             device_id_type=MESH,
         )
 
+    scalars[0].wait()
     loads[0].wait()
     groups = list(range(ranks // 2 - 1, -1, -1))
     for j in groups:
@@ -166,8 +177,8 @@
         for k in range(own):
             rank_copy(1, bases[1] + j, k).start()
 
-    loads[1].wait()
-    loads[2].wait()
+    for load in scalars[1:] + loads[1:3]:
+        load.wait()
 
     def decode(k, carry):
         one = first_in[k].astype(jnp.float32)
@@ -284,10 +295,8 @@
     lax.fori_loop(0, own, finish, 0)
     for r in range(1, experts):
         scale_copy(r).start()
-    stores = [pltpu.make_async_copy(master, new_master_out, store_sem.at[0])]
-    stores[0].start()
-
-    def encode(values, code, scale_out, power_out, k):
+
+    def encode(values, code, at, k):
         size = jnp.abs(values)
         largest = tile_max(size)
         average = tile_sum(size) * (1.0 / (side * side))
@@ -296,19 +305,15 @@
         )
         scale = largest + EPSILON
         code[k] = signed_power(values, jnp.log(size / scale), power).astype(jnp.bfloat16)
-        scale_out[k] = scale[0, 0]
-        power_out[k] = power[0, 0]
+        stats_out[at * own + k] = jnp.broadcast_to(scale, (1, side))
+        stats_out[(at + 1) * own + k] = jnp.broadcast_to(power, (1, side))
 
     def encode_both(k, carry):
-        encode(first[k], first_code, first_scale_out, first_power_out, k)
-        encode(second[k], second_code, second_scale_out, second_power_out, k)
+        encode(first[k], first_code, 0, k)
+        encode(second[k], second_code, 2, k)
         return carry
 
     lax.fori_loop(0, own, encode_both, 0)
-    stores.append(pltpu.make_async_copy(first_code, first_out, store_sem.at[1]))
-    stores.append(pltpu.make_async_copy(second_code, second_out, store_sem.at[2]))
-    stores[1].start()
-    stores[2].start()
 
     order = [0]
     for bit in expert_bits:
@@ -322,8 +327,6 @@
                     gather_copy(r, bit, k).start()
     for r in range(1, experts):
         scale_copy(r).wait_recv()
-    stores.append(pltpu.make_async_copy(weights, weight_out, store_sem.at[3]))
-    stores[3].start()
 
     for bit in bits_of(ranks):
         for j in range(ranks // (2 * bit)):
@@ -344,8 +347,52 @@
             gather_copy(r - low_bit(r), low_bit(r), k).wait_send()
     for r in range(1, experts):
         scale_copy(r).wait_send()
-    for store in stores:
-        store.wait()
+
+
+def diagonal(rows):
+    count, _, lanes = rows.shape
+    rows = rows[...].reshape(count, lanes)
+    at = lax.broadcasted_iota(jnp.int32, rows.shape, 0)
+    lane = lax.broadcasted_iota(jnp.int32, rows.shape, 1)
+    return jnp.sum(jnp.where(at == lane, rows, 0.0), axis=0)[:count]
+
+
+def write_kernel(
+    own,
+    master,
+    first_code,
+    second_code,
+    weights,
+    stats,
+    weight_scale,
+    master_out,
+    first_out,
+    first_scale_out,
+    first_power_out,
+    second_out,
+    second_scale_out,
+    second_power_out,
+    weight_out,
+    weight_scale_out,
+    sem,
+):
+    pairs = (
+        (weights, weight_out),
+        (master, master_out),
+        (first_code, first_out),
+        (second_code, second_out),
+    )
+    copies = [
+        pltpu.make_async_copy(src, dst, sem.at[i]) for i, (src, dst) in enumerate(pairs)
+    ]
+    for copy in copies:
+        copy.start()
+    outs = (first_scale_out, first_power_out, second_scale_out, second_power_out)
+    for i, out in enumerate(outs):
+        out[...] = diagonal(stats.at[pl.ds(i * own, own)])
+    weight_scale_out[...] = diagonal(weight_scale).astype(jnp.bfloat16)
+    for copy in copies:
+        copy.wait()
 
 
 def on_device(
@@ -366,43 +413,46 @@
     numel = float(own * ranks * experts * side * side)
     _, slots = slots_of(ranks)
     tiles = (own, side, side)
-    smem = pl.BlockSpec(memory_space=pltpu.SMEM)
-    vmem = pl.BlockSpec(memory_space=pltpu.VMEM)
-    hbm = pl.BlockSpec(memory_space=pl.ANY)
-    small = jax.ShapeDtypeStruct((own,), jnp.float32)
+    gathered = (experts * own, side, side)
+    smem, vmem = pltpu.SMEM, pltpu.VMEM
+    in_vmem = pl.BlockSpec(memory_space=vmem)
+    in_hbm = pl.BlockSpec(memory_space=pltpu.HBM)
+    shape = jax.ShapeDtypeStruct
+    small = shape((own,), jnp.float32)
+
+    def pin(operand):
+        return pltpu.with_memory_space_constraint(operand, pltpu.HBM)
+
     dma = pltpu.SemaphoreType.DMA
-    out = pl.pallas_call(
+    results = pl.pallas_call(
         functools.partial(kernel, ranks, experts, own, numel),
         out_shape=(
-            jax.ShapeDtypeStruct(tiles, jnp.float32),
-            jax.ShapeDtypeStruct(tiles, jnp.bfloat16),
-            jax.ShapeDtypeStruct(tiles, jnp.bfloat16),
-            jax.ShapeDtypeStruct((experts * own, side, side), jnp.bfloat16),
-            small,
-            small,
-            small,
-            small,
-            jax.ShapeDtypeStruct((experts * own, 1, side), jnp.float32),
+            vmem(tiles, jnp.float32),
+            vmem(tiles, jnp.bfloat16),
+            vmem(tiles, jnp.bfloat16),
+            vmem(gathered, jnp.bfloat16),
+            vmem((4 * own, 1, side), jnp.float32),
+            vmem((experts * own, 1, side), jnp.float32),
         ),
-        in_specs=[smem] * 6 + [hbm] * 4,
-        out_specs=(hbm,) * 4 + (smem,) * 4 + (vmem,),
+        in_specs=[in_hbm, pl.BlockSpec(memory_space=smem)] + [in_hbm] * 8,
+        out_specs=(in_vmem,) * 6,
         scratch_shapes=[
-            pltpu.VMEM((block, side, side), jnp.bfloat16),
-            pltpu.VMEM((slots * own, side, side), jnp.bfloat16),
-            pltpu.VMEM((slots * own, side, side), jnp.bfloat16),
-            pltpu.VMEM(tiles, jnp.float32),
-            pltpu.VMEM(tiles, jnp.float32),
-            pltpu.VMEM(tiles, jnp.bfloat16),
-            pltpu.VMEM(tiles, jnp.bfloat16),
-            pltpu.VMEM(tiles, jnp.float32),
-            pltpu.VMEM(tiles, jnp.float32),
-            pltpu.VMEM(tiles, jnp.bfloat16),
-            pltpu.VMEM(tiles, jnp.bfloat16),
-            pltpu.VMEM((experts * own, side, side), jnp.bfloat16),
-            pltpu.VMEM((experts, 1, side), jnp.float32),
-            pltpu.VMEM((ranks, 1, side), jnp.float32),
-            dma((4,)),
-            dma((4,)),
+            smem(owner_table.shape, jnp.int32),
+            smem((own,), jnp.float32),
+            smem((own,), jnp.float32),
+            smem((own,), jnp.float32),
+            smem((own,), jnp.float32),
+            vmem((block, side, side), jnp.bfloat16),
+            vmem((slots * own, side, side), jnp.bfloat16),
+            vmem((slots * own, side, side), jnp.bfloat16),
+            vmem(tiles, jnp.float32),
+            vmem(tiles, jnp.bfloat16),
+            vmem(tiles, jnp.bfloat16),
+            vmem(tiles, jnp.float32),
+            vmem(tiles, jnp.float32),
+            vmem((experts, 1, side), jnp.float32),
+            vmem((ranks, 1, side), jnp.float32),
+            dma((10,)),
             dma((slots,)),
             dma((slots * own,)),
             dma((experts + ranks - 2,)),
@@ -416,30 +466,45 @@
             collective_id=0, has_side_effects=True, vmem_limit_bytes=48 << 20
         ),
     )(
-        owner_table,
+        pin(owner_table),
         step_count,
-        first_scale,
-        first_power,
-        second_scale,
-        second_power,
-        gradients,
-        master,
-        first_code,
-        second_code,
+        pin(first_scale),
+        pin(first_power),
+        pin(second_scale),
+        pin(second_power),
+        pin(gradients),
+        pin(master),
+        pin(first_code),
+        pin(second_code),
     )
-    new_master, first_new, second_new, weights = out[:4]
-    scales = out[8][:, 0, 0].astype(jnp.bfloat16)
-    return (
-        new_master,
-        first_new,
-        out[4],
-        out[5],
-        second_new,
-        out[6],
-        out[7],
-        weights,
-        scales,
-    )
+    return pl.pallas_call(
+        functools.partial(write_kernel, own),
+        out_shape=(
+            pltpu.HBM(tiles, jnp.float32),
+            pltpu.HBM(tiles, jnp.bfloat16),
+            small,
+            small,
+            pltpu.HBM(tiles, jnp.bfloat16),
+            small,
+            small,
+            pltpu.HBM(gathered, jnp.bfloat16),
+            shape((experts * own,), jnp.bfloat16),
+        ),
+        in_specs=[in_vmem] * 6,
+        out_specs=(
+            in_hbm,
+            in_hbm,
+            in_vmem,
+            in_vmem,
+            in_hbm,
+            in_vmem,
+            in_vmem,
+            in_hbm,
+            in_vmem,
+        ),
+        scratch_shapes=[dma((4,))],
+        compiler_params=pltpu.CompilerParams(vmem_limit_bytes=16 << 20),
+    )(*results)
 
 
 def solution(mesh):

time: 45.3 us -> 34.5 us (0.76)
  local copies, waits for them, and re-layouts: 10.9 us -> 0 us
    unnamed x26 -> x0, local copies, waits for them, and re-layouts: 10.1 us -> none
    pallas_call x0 -> x1, Pallas kernels: none -> 1.52 us  [on_device(): pl.pallas_call(functools.partial(write_kernel, own), out_shape=(pltpu.HBM...]
    pallas_call x1, Pallas kernels: 32.8 us -> 31.5 us  [on_device(): pl.pallas_call(functools.partial(kernel, ranks, experts, own, numel), out...]
    slice x1 -> x0, local copies, waits for them, and re-layouts: 0.71 us -> none  [on_device(): scales = out[8][:, 0, 0].astype(jnp.bfloat16)]
where the time goes in v2:
time: 34.5 us; the launch traced here: 34.3 us
  Pallas kernels  33 us (96%)
  between operations  1.3 us (4%)
    pallas_call x1, Pallas kernels, on_device(): pl.pallas_call(functools.partial(kernel, ranks, experts, own, numel), out...  31.5 us
    pallas_call x1, Pallas kernels, on_device(): pl.pallas_call(functools.partial(write_kernel, own), out_shape=(pltpu.HBM...  1.52 us

profile of v2, /device:TPU:0, one launch (start us, length us, event | category | flops | bytes accessed | tf_op | source)
XLA Modules:
  0.0 34.3 jit_solution(11622857025674401296)
XLA Ops:
  1.3 31.5 %shard_map.169 = (f32[4,128,128]{2,1,0:T(8,128)S(1)}, bf16[4,128,128]{2,1,0:T(8,128)(2,1)S(1)}, bf16[4,128,128]{2,1,0:T(8,128)(2,1)S(1)}, bf16[16,128,128]{2,1,0...) custom-call(s32[1,32]{1,0:T(1,128)} %table_hbm.1, s32[1]{0:T(128)S(6)} %copy.19.step_count, ...), custom_call_target="tpu_custom_call" | custom-call | tf_op jit(solution)/shard_map/pallas_call | solution.py:427
  32.8 1.5 %shard_map.170 = (f32[4,128,128]{2,1,0:T(8,128)}, bf16[4,128,128]{2,1,0:T(8,128)(2,1)}, f32[4]{0:T(128)}, f32[4]{0:T(128)}, bf16[4,128,128]{2,1,0:T(8,128)(2,1)}...) custom-call(f32[4,128,128]{2,1,0:T(8,128)S(1)} %get-tuple-element.15.master, ...), custom_call_target="tpu_custom_call" | custom-call | tf_op jit(solution)/shard_map/pallas_call | solution.py:480

commit v3 on v2

--- a/solution.py
+++ b/solution.py
@@ -98,8 +98,7 @@
     second_in,
     first,
     second,
-    sums_expert,
-    sums_rank,
+    sums,
     load_sem,
     send_sem,
     recv_sem,
@@ -137,13 +136,13 @@
     loads[0].start()
 
     barrier = pltpu.get_barrier_semaphore()
-    for r in range(1, ranks):
+    peers = [(i // experts, i % experts) for i in range(ranks * experts - 1, 0, -1)]
+    for r, q in peers:
         pl.semaphore_signal(
-            barrier, inc=1, device_id=(flip(me, r), expert), device_id_type=MESH
-        )
-    for r in range(1, experts):
-        pl.semaphore_signal(
-            barrier, inc=1, device_id=(me, flip(expert, r)), device_id_type=MESH
+            barrier,
+            inc=1,
+            device_id=(flip(me, r), flip(expert, q)),
+            device_id_type=MESH,
         )
     for load in scalars[1:] + loads[1:]:
         load.start()
@@ -172,7 +171,7 @@
             return carry
 
         lax.fori_loop(0, own, place, 0)
-    pl.semaphore_wait(barrier, ranks + experts - 2)
+    pl.semaphore_wait(barrier, len(peers))
     for j in groups:
         for k in range(own):
             rank_copy(1, bases[1] + j, k).start()
@@ -215,39 +214,28 @@
 
         square = lax.fori_loop(0, own, add, square)
 
-    def sum_copy(buffer, at, slot, target):
+    def sum_copy(src, dst, r, q):
         return pltpu.make_async_remote_copy(
-            src_ref=buffer.at[0],
-            dst_ref=buffer.at[at],
-            send_sem=sum_send.at[slot],
-            recv_sem=sum_recv.at[slot],
-            device_id=target,
+            src_ref=sums.at[src],
+            dst_ref=sums.at[dst],
+            send_sem=sum_send,
+            recv_sem=sum_recv,
+            device_id=(flip(me, r), flip(expert, q)),
             device_id_type=MESH,
         )
 
-    expert_sums = [
-        sum_copy(sums_expert, r, r - 1, (me, flip(expert, r))) for r in range(1, experts)
-    ]
-    rank_sums = [
-        sum_copy(sums_rank, r, experts - 2 + r, (flip(me, r), expert))
-        for r in range(1, ranks)
-    ]
-    sums_expert[0] = jnp.sum(square, axis=0, keepdims=True)
-    for copy in expert_sums:
-        copy.start()
-    for copy in expert_sums:
-        copy.wait_recv()
-    sums_rank[0] = jnp.sum(sums_expert[...], axis=0)
-    for copy in rank_sums:
-        copy.start()
+    sums[0] = jnp.sum(square, axis=0, keepdims=True)
+    for r, q in peers:
+        sum_copy(0, r * experts + q, r, q).start()
+    others = pl.ds(1, len(peers))
+    all_sums = sum_copy(others, others, *peers[0])
 
     loads[3].wait()
     steps = jnp.full((1, side), step_count[0].astype(jnp.float32), jnp.float32)
-    bias_one = (1.0 - jnp.exp(steps * math.log(BETA_ONE)))[:, :1]
-    bias_two = (1.0 - jnp.exp(steps * math.log(BETA_TWO)))[:, :1]
-    for copy in rank_sums:
-        copy.wait_recv()
-    total_sq = jnp.sum(jnp.sum(sums_rank[...], axis=0), axis=1, keepdims=True)
+    unbias_one = (1.0 / (1.0 - jnp.exp(steps * math.log(BETA_ONE))))[:, :1]
+    unbias_two = (1.0 / (1.0 - jnp.exp(steps * math.log(BETA_TWO))))[:, :1]
+    all_sums.wait_recv()
+    total_sq = jnp.sum(jnp.sum(sums[...], axis=0), axis=1, keepdims=True)
     clip_factor = jnp.minimum(1.0, CLIP_RMS / jnp.sqrt(total_sq / numel + EPSILON))
 
     def gather_copy(r, bit, k):
@@ -275,45 +263,45 @@
 
     expert_bits = bits_of(experts)[::-1]
 
-    def finish(k, carry):
+    largest = []
+    for k in range(own):
         grad = acc[k] * clip_factor
         one = first[k] + (1.0 - BETA_ONE) * grad
         two = second[k] + (1.0 - BETA_TWO) * grad * grad
         first[k] = one
         second[k] = two
-        update = one / bias_one / (jnp.sqrt(two / bias_two) + ADAM_EPS)
+        update = (one * unbias_one) / (jnp.sqrt(two * unbias_two) + ADAM_EPS)
         old = master[k]
         new = old - LEARN_RATE * (update + WEIGHT_DECAY * old)
         master[k] = new
-        scale = (tile_max(jnp.abs(new)) + EPSILON).astype(jnp.bfloat16).astype(jnp.float32)
-        weights[expert * own + k] = (new / scale).astype(jnp.bfloat16)
+        largest.append(tile_max(jnp.abs(new)))
+    for k in range(own):
+        scale = (largest[k] + EPSILON).astype(jnp.bfloat16).astype(jnp.float32)
+        weights[expert * own + k] = (master[k] * (1.0 / scale)).astype(jnp.bfloat16)
         weight_scale_out[expert * own + k] = jnp.broadcast_to(scale, (1, side))
         for bit in expert_bits:
             gather_copy(0, bit, k).start()
-        return carry
-
-    lax.fori_loop(0, own, finish, 0)
     for r in range(1, experts):
         scale_copy(r).start()
 
-    def encode(values, code, at, k):
-        size = jnp.abs(values)
+    moments = [(ref, code, at, k) for k in range(own)
+               for ref, code, at in ((first, first_code, 0), (second, second_code, 2))]
+    ranges = []
+    for ref, _, at, k in moments:
+        size = jnp.abs(ref[k])
         largest = tile_max(size)
         average = tile_sum(size) * (1.0 / (side * side))
         power = jnp.clip(
             LOG_SPAN / jnp.log(1.0 + largest / (average + EPSILON)), 1.0, 3.0
         )
         scale = largest + EPSILON
-        code[k] = signed_power(values, jnp.log(size / scale), power).astype(jnp.bfloat16)
         stats_out[at * own + k] = jnp.broadcast_to(scale, (1, side))
         stats_out[(at + 1) * own + k] = jnp.broadcast_to(power, (1, side))
-
-    def encode_both(k, carry):
-        encode(first[k], first_code, 0, k)
-        encode(second[k], second_code, 2, k)
-        return carry
-
-    lax.fori_loop(0, own, encode_both, 0)
+        ranges.append((1.0 / scale, power))
+    for (ref, code, _, k), (shrink, power) in zip(moments, ranges):
+        values = ref[k]
+        logs = jnp.log(jnp.abs(values) * shrink)
+        code[k] = signed_power(values, logs, power).astype(jnp.bfloat16)
 
     order = [0]
     for bit in expert_bits:
@@ -340,8 +328,7 @@
                 device_id=(flip(me, bit), expert),
                 device_id_type=MESH,
             ).wait_send()
-    for copy in expert_sums + rank_sums:
-        copy.wait_send()
+    all_sums.wait_send()
     for r in order[1:]:
         for k in range(own):
             gather_copy(r - low_bit(r), low_bit(r), k).wait_send()
@@ -450,13 +437,12 @@
             vmem(tiles, jnp.bfloat16),
             vmem(tiles, jnp.float32),
             vmem(tiles, jnp.float32),
-            vmem((experts, 1, side), jnp.float32),
-            vmem((ranks, 1, side), jnp.float32),
+            vmem((ranks * experts, 1, side), jnp.float32),
             dma((10,)),
             dma((slots,)),
             dma((slots * own,)),
-            dma((experts + ranks - 2,)),
-            dma((experts + ranks - 2,)),
+            dma,
+            dma,
             dma(((experts - 1) * own,)),
             dma(((experts - 1) * own,)),
             dma((experts - 1,)),

time: 34.5 us -> 34.9 us (1.012)
  Pallas kernels: 33 us -> 33.4 us
    pallas_call x1, Pallas kernels: 31.5 us -> 31.9 us  [on_device(): pl.pallas_call(functools.partial(kernel, ranks, experts, own, numel), out...]
where the time goes in v3:
time: 34.9 us; the launch traced here: 34.7 us
  Pallas kernels  33.4 us (96%)
  between operations  1.3 us (4%)
    pallas_call x1, Pallas kernels, on_device(): pl.pallas_call(functools.partial(kernel, ranks, experts, own, numel), out...  31.9 us
    pallas_call x1, Pallas kernels, on_device(): pl.pallas_call(functools.partial(write_kernel, own), out_shape=(pltpu.HBM...  1.52 us

profile of v3, /device:TPU:0, one launch (start us, length us, event | category | flops | bytes accessed | tf_op | source)
XLA Modules:
  0.0 34.7 jit_solution(17554384886870454326)
XLA Ops:
  1.3 31.9 %shard_map.169 = (f32[4,128,128]{2,1,0:T(8,128)S(1)}, bf16[4,128,128]{2,1,0:T(8,128)(2,1)S(1)}, bf16[4,128,128]{2,1,0:T(8,128)(2,1)S(1)}, bf16[16,128,128]{2,1,0...) custom-call(s32[1,32]{1,0:T(1,128)} %table_hbm.1, s32[1]{0:T(128)S(6)} %copy.19.step_count, ...), custom_call_target="tpu_custom_call" | custom-call | tf_op jit(solution)/shard_map/pallas_call | solution.py:414
  33.2 1.5 %shard_map.170 = (f32[4,128,128]{2,1,0:T(8,128)}, bf16[4,128,128]{2,1,0:T(8,128)(2,1)}, f32[4]{0:T(128)}, f32[4]{0:T(128)}, bf16[4,128,128]{2,1,0:T(8,128)(2,1)}...) custom-call(f32[4,128,128]{2,1,0:T(8,128)S(1)} %get-tuple-element.15.master, ...), custom_call_target="tpu_custom_call" | custom-call | tf_op jit(solution)/shard_map/pallas_call | solution.py:466
